TPU v7x, 256 devices: a 2x2x32 block of a 4x8x32 slice. The times are simulated.
256 devices in a mesh: group: 4 (over y, x), blk: 64 (over z, core).
Axes of the slice: x: 2, y: 2, z: 32, core: 2. Of those that a mesh axis runs over, the one named last changes fastest.
The devices are a block of a 4x8x32 slice.
Arguments:
- queries: bfloat16 [8, 256, 2048], P('group', 'blk'), parts along dimension 0, may hold values from -160 to 160
- keys: bfloat16 [8, 81920, 256], P('group', 'blk'), parts along dimension 0, may hold values from -4 to 4
- values: bfloat16 [8, 81920, 256], P('group', 'blk'), parts along dimension 0, may hold values from -6 to 6
- lengths: int32 [8], P('group'), parts along dimension 0, may hold values from 61440 to 81920
- offsets: int32 [8], P('group'), parts along dimension 0, may hold values from 51200 to 81664
Outputs:
- attended: bfloat16 [8, 256, 2048], P('group', 'blk'), parts along dimension 0
There are 4 independent parts, one for each index of `group`. A program takes and returns all parts, laid end to end along the dimension named above; each array names one. Nothing has to cross between parts.
All inputs are finite; a program needn't handle non-finite values.
Results may differ from a plain program's by a relative error of at most 0.0085.
Values may be sent and summed in bfloat16 or wider, within the bound.
A program may use at most 64 MiB of HBM per device.

v0:
```python
import math

import jax
import jax.numpy as jnp
from jax import lax
from jax.sharding import PartitionSpec as P

KV_HEADS = 2
HEAD_DIM = 128


masked_low = -1e30


def shard_partial(query_rows, key_rows, value_rows, query_pos, key_pos, lengths):
    micro_count, rows_count, row_width = query_rows.shape
    heads_count = row_width // HEAD_DIM
    group_size = heads_count // KV_HEADS
    query_split = query_rows.reshape(micro_count, rows_count, KV_HEADS, group_size, HEAD_DIM)
    key_split = key_rows.reshape(micro_count, key_rows.shape[1], KV_HEADS, HEAD_DIM)
    value_split = value_rows.reshape(micro_count, value_rows.shape[1], KV_HEADS, HEAD_DIM)
    scores = jnp.einsum(
        "brkgd,bskd->bkgrs", query_split, key_split, preferred_element_type=jnp.float32
    )
    scores = scores * (1.0 / math.sqrt(HEAD_DIM))
    visible = (key_pos[None, None, :] <= query_pos[:, :, None]) & (
        key_pos[None, None, :] < lengths[:, None, None]
    )
    visible = visible[:, None, None, :, :]
    any_visible = jnp.any(visible, axis=-1)
    row_max = jnp.max(jnp.where(visible, scores, masked_low), axis=-1)
    safe_max = jnp.where(any_visible, row_max, 0.0)
    shifted = jnp.where(visible, scores - safe_max[..., None], 0.0)
    weights = jnp.where(visible, jnp.exp(shifted), 0.0)
    totals = jnp.sum(weights, axis=-1)
    bounded = jnp.maximum(totals, 1.0)
    numerator = jnp.einsum(
        "bkgrs,bskd->bkgrd",
        weights.astype(jnp.bfloat16),
        value_split,
        preferred_element_type=jnp.float32,
    )
    partial_value = (numerator / bounded[..., None]).astype(jnp.bfloat16)
    partial_value = jnp.transpose(partial_value, (0, 3, 1, 2, 4)).reshape(
        micro_count, rows_count, row_width
    )
    logsum = jnp.where(any_visible, safe_max + jnp.log(bounded), masked_low)
    logsum = jnp.transpose(logsum, (0, 3, 1, 2)).reshape(micro_count, rows_count, heads_count)
    return (partial_value, logsum)


def body(queries, keys, values, lengths, offsets):
    micro_count, local_rows, row_width = queries.shape
    local_keys = keys.shape[1]
    heads_count = row_width // HEAD_DIM
    shards = lax.axis_size("blk")
    key_pos = lax.axis_index("blk") * local_keys + jnp.arange(local_keys, dtype=jnp.int32)
    visiting = lax.all_gather(queries, "blk", axis=1, tiled=True)
    rows_count = visiting.shape[1]
    block_rows = math.gcd(rows_count, 64)
    block_count = rows_count // block_rows

    def one_block(block_index):
        block_start = block_index * block_rows
        selected = lax.dynamic_slice_in_dim(visiting, block_start, block_rows, 1)
        query_pos = (
            offsets[:, None] + block_start + jnp.arange(block_rows, dtype=jnp.int32)[None, :]
        )
        return shard_partial(selected, keys, values, query_pos, key_pos, lengths)

    block_parts, block_logs = lax.map(one_block, jnp.arange(block_count, dtype=jnp.int32))
    block_parts = jnp.moveaxis(block_parts, 0, 1).reshape(micro_count, rows_count, row_width)
    block_logs = jnp.moveaxis(block_logs, 0, 1).reshape(micro_count, rows_count, heads_count)
    partials = block_parts
    logsums = block_logs
    partials, logsums = (partials, logsums)
    shaped_parts = partials.reshape(micro_count, shards, local_rows, row_width)
    shaped_logs = logsums.reshape(micro_count, shards, local_rows, heads_count)
    home_parts = lax.all_to_all(shaped_parts, "blk", split_axis=1, concat_axis=1, tiled=True)
    home_logs = lax.all_to_all(shaped_logs, "blk", split_axis=1, concat_axis=1, tiled=True)
    row_peak = jnp.max(home_logs, axis=1, keepdims=True)
    scales = jnp.exp(home_logs - row_peak)
    denominator = jnp.sum(scales, axis=1)
    split_parts = home_parts.reshape(micro_count, shards, local_rows, heads_count, HEAD_DIM)
    weighted = jnp.sum(split_parts * scales[..., None], axis=1)
    merged = weighted / denominator[..., None]
    attended = merged.reshape(micro_count, local_rows, row_width).astype(jnp.bfloat16)
    return attended


def solution(mesh):
    return jax.shard_map(
        body,
        mesh=mesh,
        in_specs=(
            P("group", "blk", None),
            P("group", "blk", None),
            P("group", "blk", None),
            P("group"),
            P("group"),
        ),
        out_specs=P("group", "blk", None),
        check_vma=False,
    )
```

profile of v0, /device:TPU:37, one launch (start us, length us, event | category | flops | bytes accessed | tf_op | source)
XLA Modules:
  0.0 481.0 jit_solution(16185152529671269494)
XLA Ops:
  8.1 3.8 reshape.97
  11.9 2.9 reshape.98
  14.9 139.4 %all-gather.2.cloned.1.call-done = bf16[2,256,2048]{2,0,1:T(2,128)(2,1)} async-done(((bf16[2,4,2048]{2,0,1:T(2,128)(2,1)}), bf16[2,256,2048]{2,0,1:T(2,128)(2,1)}) %all-gather.2.cloned.1.call-update) | async-done | bytes 2097168 | tf_op jit(solution)/shard_map/all_gather | solution.py:58
  154.3 71.4 %while.14 = (s32[]{:T(128)}, bf16[4,2,64,2048]{3,2,1,0:T(8,128)(2,1)}, f32[4,2,64,16]{2,3,1,0:T(8,128)S(1)}, s32[4]{0:T(128)S(1)}, s32[2]{0:T(128)S(1)}, /*index...) while((s32[]{:T(128)}, ...), condition=%wide.wide.region_4.5_spmd.clone, body=%wide.wide.region_0.4_spmd.clone.sunk | while | flops 1377611520 | bytes 88389816 | solution.py:71
  157.6 3.0 fusion.38
  161.0 4.3 fusion.39
  165.5 5.4 %divide_convert_fusion.4 = bf16[2,64,2,8,128]{4,3,1,2,0:T(8,128)(2,1)S(1)} fusion(bf16[2,1280,2,128,1]{3,2,1,0,4:T(2,128)(2,1)S(1)} %bitcast.95, f32[2,2,64,8,1280]{4,3,2,1,0:T(8,128)} %copy-done, f32[2,2,8,64]{2,3,1,0:T(8,128)S(1)} %broadcast_select_fusion.3, pred[2,64,1280]{2,1,0:T(8,128)(4,1)S(1)} %compare_and_fusion.3, ...), kind=kOutput, calls=%fused_computation.15.clone.clone.1 | convolution fusion | flops 684720128 | bytes 12500992 | tf_op jit(solution)/shard_map/while/body/eval_jaxpr/bkgrs,bskd->bkgrd/dot_general | solution.py:37
  175.5 3.0 fusion.38
  178.8 4.3 fusion.39
  183.4 5.4 %divide_convert_fusion.4 = bf16[2,64,2,8,128]{4,3,1,2,0:T(8,128)(2,1)S(1)} fusion(bf16[2,1280,2,128,1]{3,2,1,0,4:T(2,128)(2,1)S(1)} %bitcast.95, f32[2,2,64,8,1280]{4,3,2,1,0:T(8,128)} %copy-done, f32[2,2,8,64]{2,3,1,0:T(8,128)S(1)} %broadcast_select_fusion.3, pred[2,64,1280]{2,1,0:T(8,128)(4,1)S(1)} %compare_and_fusion.3, ...), kind=kOutput, calls=%fused_computation.15.clone.clone.1 | convolution fusion | flops 684720128 | bytes 12500992 | tf_op jit(solution)/shard_map/while/body/eval_jaxpr/bkgrs,bskd->bkgrd/dot_general | solution.py:37
  193.4 3.0 fusion.38
  196.7 4.3 fusion.39
  201.3 5.4 %divide_convert_fusion.4 = bf16[2,64,2,8,128]{4,3,1,2,0:T(8,128)(2,1)S(1)} fusion(bf16[2,1280,2,128,1]{3,2,1,0,4:T(2,128)(2,1)S(1)} %bitcast.95, f32[2,2,64,8,1280]{4,3,2,1,0:T(8,128)} %copy-done, f32[2,2,8,64]{2,3,1,0:T(8,128)S(1)} %broadcast_select_fusion.3, pred[2,64,1280]{2,1,0:T(8,128)(4,1)S(1)} %compare_and_fusion.3, ...), kind=kOutput, calls=%fused_computation.15.clone.clone.1 | convolution fusion | flops 684720128 | bytes 12500992 | tf_op jit(solution)/shard_map/while/body/eval_jaxpr/bkgrs,bskd->bkgrd/dot_general | solution.py:37
  211.2 3.0 fusion.38
  214.5 4.3 fusion.39
  219.1 5.4 %divide_convert_fusion.4 = bf16[2,64,2,8,128]{4,3,1,2,0:T(8,128)(2,1)S(1)} fusion(bf16[2,1280,2,128,1]{3,2,1,0,4:T(2,128)(2,1)S(1)} %bitcast.95, f32[2,2,64,8,1280]{4,3,2,1,0:T(8,128)} %copy-done, f32[2,2,8,64]{2,3,1,0:T(8,128)S(1)} %broadcast_select_fusion.3, pred[2,64,1280]{2,1,0:T(8,128)(4,1)S(1)} %compare_and_fusion.3, ...), kind=kOutput, calls=%fused_computation.15.clone.clone.1 | convolution fusion | flops 684720128 | bytes 12500992 | tf_op jit(solution)/shard_map/while/body/eval_jaxpr/bkgrs,bskd->bkgrd/dot_general | solution.py:37
  226.7 13.8 %all-to-all-start.1 = ((f32[64,1,128]{2,1,0:T(1,128)}), f32[64,1,128]{2,1,0:T(1,128)S(1)}, u32[]{:S(2)}, u32[]{:S(2)}) async-start(f32[64,1,128]{2,1,0:T(1,128)} %reshape.95), calls=%async_computation.1 | async-start | bytes 65536 | tf_op jit(solution)/shard_map/all_to_all | solution.py:80
  240.5 5.1 %copy.53 = bf16[2,4,64,2048]{3,0,2,1:T(2,128)(2,1)} copy(bf16[2,4,64,2048]{3,2,0,1:T(8,128)(2,1)} %bitcast.94) | data formatting | bytes 4194304 | tf_op jit(solution)/shard_map/transpose | solution.py:72
  245.6 16.6 %all-to-all-done.1 = f32[64,1,128]{2,1,0:T(1,128)S(1)} async-done(((f32[64,1,128]{2,1,0:T(1,128)}), f32[64,1,128]{2,1,0:T(1,128)S(1)}, u32[]{:S(2)}, u32[]{:S(2)}) %all-to-all-start.1) | async-done | bytes 32800 | tf_op jit(solution)/shard_map/all_to_all | solution.py:80
  262.2 6.6 %all-to-all-start = ((bf16[2,64,4,2048]{3,0,2,1:T(2,128)(2,1)}), bf16[2,64,4,2048]{3,0,2,1:T(2,128)(2,1)S(1)}, u32[]{:S(2)}, u32[]{:S(2)}) async-start(bf16[2,64,4,2048]{3,0,2,1:T(2,128)(2,1)} %bitcast.93), calls=%async_computation | async-start | bytes 4194304 | tf_op jit(solution)/shard_map/all_to_all | solution.py:79
  270.7 2.6 mul.27
  273.3 5.8 %mul.28 = f32[2,64,4,2048]{3,0,2,1:T(2,128)} reshape(f32[2,64,4,16,128]{4,3,0,2,1:T(8,128)} %mul.27) | data formatting | bytes 8388608 | tf_op jit(solution)/shard_map/mul | solution.py:85
  279.2 189.7 %all-to-all-done = bf16[2,64,4,2048]{3,0,2,1:T(2,128)(2,1)S(1)} async-done(((bf16[2,64,4,2048]{3,0,2,1:T(2,128)(2,1)}), bf16[2,64,4,2048]{3,0,2,1:T(2,128)(2,1)S(1)}, u32[]{:S(2)}, u32[]{:S(2)}) %all-to-all-start) | async-done | bytes 2097184 | tf_op jit(solution)/shard_map/all_to_all | solution.py:79
  468.9 4.5 multiply_reduce_fusion
  (108 shorter events, 22.6 us)
Async XLA Ops:
  6.5 147.7 %copy-start.2 = (s32[2]{0:T(128)S(1)}, s32[2]{0:T(128)}, u32[]{:S(2)}) copy-start(s32[2]{0:T(128)} %param.10) | copy-start | bytes 28
  6.5 147.7 %copy-start.3 = (s32[2]{0:T(128)S(1)}, s32[2]{0:T(128)}, u32[]{:S(2)}) copy-start(s32[2]{0:T(128)} %param.11) | copy-start | bytes 28
  6.6 147.7 %all-gather.2.cloned.1.call-start = ((), (), s32[]{:S(2)}) async-start(), calls=%async_computation.2 | async-start | bytes 2129920 | tf_op jit(solution)/shard_map/all_gather | solution.py:58
  160.6 4.7 copy-start
  161.0 4.5 copy-start.1
  178.5 4.7 copy-start
  178.8 4.5 copy-start.1
  196.3 4.7 copy-start
  196.7 4.5 copy-start.1
  214.2 4.7 copy-start
  214.5 4.5 copy-start.1
  226.7 35.6 %all-to-all-start.1 = ((f32[64,1,128]{2,1,0:T(1,128)}), f32[64,1,128]{2,1,0:T(1,128)S(1)}, u32[]{:S(2)}, u32[]{:S(2)}) async-start(f32[64,1,128]{2,1,0:T(1,128)} %reshape.95), calls=%async_computation.1 | async-start | bytes 65536 | tf_op jit(solution)/shard_map/all_to_all | solution.py:80
  262.2 206.7 %all-to-all-start = ((bf16[2,64,4,2048]{3,0,2,1:T(2,128)(2,1)}), bf16[2,64,4,2048]{3,0,2,1:T(2,128)(2,1)S(1)}, u32[]{:S(2)}, u32[]{:S(2)}) async-start(bf16[2,64,4,2048]{3,0,2,1:T(2,128)(2,1)} %bitcast.93), calls=%async_computation | async-start | bytes 4194304 | tf_op jit(solution)/shard_map/all_to_all | solution.py:79
Sparse Core Ops, SparseCore 0:
  9.2 145.0 all-gather.1
where the time goes:
time: 482 us; the launch traced here: 481 us
  waiting for transfers between devices  346 us (72%)
  local copies, waits for them, and re-layouts  38.7 us (8%)
  matrix products  33.6 us (7%)
  other arithmetic  26 us (5%)
  starting transfers between devices  20.4 us (4%)
  between operations  13.5 us (3%)
    all_to_all x1, waiting for transfers between devices, body(): lax.all_to_all(shaped_parts, 'blk', split_axis=1, concat_axis=1, tiled=True)  190 us
    all_gather x1, waiting for transfers between devices, body(): visiting = lax.all_gather(queries, 'blk', axis=1, tiled=True)  139 us
    dot_general x4, matrix products, shard_partial(): jnp.einsum('bkgrs,bskd->bkgrd', weights.astype(jnp.bfloat16), value_split...  21.7 us
    reduce_sum x4, other arithmetic, shard_partial(): totals = jnp.sum(weights, axis=-1)  17.2 us
    all_to_all x1, waiting for transfers between devices, body(): lax.all_to_all(shaped_logs, 'blk', split_axis=1, concat_axis=1, tiled=True)  16.6 us
    all_to_all x1, starting transfers between devices, body(): lax.all_to_all(shaped_logs, 'blk', split_axis=1, concat_axis=1, tiled=True)  13.8 us
    dot_general x4, matrix products, shard_partial(): jnp.einsum('brkgd,bskd->bkgrs', query_split, key_split, preferred_element...  11.8 us
  transfers between devices with their start and end apart: 3, of which 3 were waited for; matrix products, arithmetic and copies ran while one was open for 5% of the time, Pallas kernels for 0%

commit v1 on v0

v1 whole, which is shorter than its diff:
```python
import functools
import math

import jax
import jax.numpy as jnp
from jax import lax
from jax.experimental import pallas as pl
from jax.experimental.pallas import tpu as pltpu
from jax.sharding import PartitionSpec as P

KV_HEADS = 2
HEAD_DIM = 128
CORES = 2
MESH = pl.DeviceIdType.MESH
EXP_SCALE = math.log2(math.e) / math.sqrt(HEAD_DIM)
LOW = -1e30
TILE = 256


def step_of(distance, strides):
    for stride in strides:
        if distance % stride == 0:
            return stride
    return 1


def merge(parts):
    best = functools.reduce(jnp.maximum, [part[1] for part in parts])
    scales = [jnp.exp2((part[1] - best) * EXP_SCALE) for part in parts]
    numer = sum(part[0].astype(jnp.float32) * scale for part, scale in zip(parts, scales))
    total = sum(part[2] * scale for part, scale in zip(parts, scales))
    return numer, best, total


def attend(keys, values_t, rows, limit):
    width = rows.shape[0]
    position = lax.broadcasted_iota(jnp.int32, (TILE, width), 0)
    best = numer = total = None
    for tile in range(keys.shape[0] // TILE):
        here = slice(tile * TILE, (tile + 1) * TILE)
        scores = lax.dot_general(
            keys[here, :], rows, (((1,), (1,)), ((), ())), preferred_element_type=jnp.float32
        )
        scores = jnp.where(position < limit - tile * TILE, scores, LOW)
        largest = scores.reshape(TILE // 8, 8, width).max(0).max(0, keepdims=True)
        newest = largest if best is None else jnp.maximum(best, largest)
        weights = jnp.exp2((scores - newest) * EXP_SCALE)
        sums = weights.reshape(TILE // 8, 8, width).sum(0)
        product = jnp.dot(
            values_t[:, here], weights.astype(jnp.bfloat16), preferred_element_type=jnp.float32
        )
        if best is None:
            numer, total = product, sums
        else:
            keep = jnp.exp2((best - newest) * EXP_SCALE)
            numer, total = numer * keep + product, total * keep + sums
        best = newest
    return numer, best, total.sum(0, keepdims=True)


def kernel(
    chips,
    heads,
    strides,
    lengths,
    offsets,
    q_in,
    k_in,
    v_in,
    out,
    keys,
    values,
    values_t,
    pick,
    q_all,
    part,
    stat,
    send,
    got,
    got_stat,
    home,
    home_got,
    local_sem,
    pair_send,
    pair_recv,
    q_send,
    q_recv,
    o_send,
    o_recv,
    s_send,
    s_recv,
):
    half = chips // 2
    group = lax.axis_index("group")
    me = lax.axis_index("blk")
    core = lax.rem(me, CORES)
    other = 1 - core
    chip = lax.div(me, CORES)
    shard = k_in.shape[1]
    rows_half = q_in.shape[1]
    columns = CORES * rows_half

    def device(z, on):
        return (group, lax.rem(z + chips, chips) * CORES + on)

    partner = device(chip, other)

    barrier = pltpu.get_barrier_semaphore()
    pl.semaphore_signal(barrier, inc=1, device_id=partner, device_id_type=MESH)
    for stride in strides:
        for way in (-1, 1):
            pl.semaphore_signal(
                barrier, inc=1, device_id=device(chip + way * stride, core), device_id_type=MESH
            )
    my_rows = pl.ds(pl.multiple_of(core * shard, 256), shard)
    my_half = pl.ds(pl.multiple_of(core * rows_half, 64), rows_half)
    locals_ = [
        pltpu.make_async_copy(q_in.at[core], q_all.at[0, 0, my_half], local_sem.at[0]),
        pltpu.make_async_copy(v_in.at[core], values.at[my_rows], local_sem.at[1]),
        pltpu.make_async_copy(k_in.at[core], keys.at[my_rows], local_sem.at[2]),
    ]
    for copy in locals_:
        copy.start()
    pl.semaphore_wait(barrier, 1 + 2 * len(strides))

    def to_partner(src, dst, index):
        return pltpu.make_async_remote_copy(
            src_ref=src,
            dst_ref=dst,
            send_sem=pair_send.at[index],
            recv_sem=pair_recv.at[index],
            device_id=partner,
            device_id_type=MESH,
        )

    swaps = [
        to_partner(q_in.at[other], q_all.at[0, 0, my_half], 0),
        to_partner(v_in.at[other], values.at[my_rows], 1),
        to_partner(k_in.at[other], keys.at[my_rows], 2),
    ]
    for copy in swaps:
        copy.start()

    row = lax.broadcasted_iota(jnp.int32, (columns, HEAD_DIM), 0)
    low = (lax.rem(row, heads) < heads // KV_HEADS).astype(jnp.float32)
    pick[0] = low.astype(jnp.bfloat16)
    pick[1] = (1.0 - low).astype(jnp.bfloat16)

    def relay(way, k, stride, src):
        slot = k + stride
        return pltpu.make_async_remote_copy(
            src_ref=src,
            dst_ref=q_all.at[way, slot],
            send_sem=q_send.at[way, slot],
            recv_sem=q_recv.at[way, slot],
            device_id=device(chip + (1 - 2 * way) * stride, core),
            device_id_type=MESH,
        )

    def arrival(way, k):
        return pltpu.make_async_remote_copy(
            src_ref=q_all.at[way, k],
            dst_ref=q_all.at[way, k],
            send_sem=q_send.at[way, k],
            recv_sem=q_recv.at[way, k],
            device_id=partner,
            device_id_type=MESH,
        )

    locals_[0].wait()
    swaps[0].wait()
    for stride in strides:
        for way in (0, 1):
            relay(way, 0, stride, q_all.at[0, 0]).start()
    q_all[1, half] = q_all[0, 0]

    locals_[1].wait()
    swaps[1].wait()
    for tile in range(values.shape[0] // TILE):
        here = slice(tile * TILE, (tile + 1) * TILE)
        values_t[:, here] = values[here, :].T
    locals_[2].wait()
    swaps[2].wait()

    length = lengths[core]
    offset = offsets[core]
    base = chip * CORES * shard
    column = lax.broadcasted_iota(jnp.int32, (1, columns), 1)
    head_low = lax.rem(column, heads) < heads // KV_HEADS

    def limit_of(source):
        position = offset + source * (columns // heads) + lax.div(column, heads)
        return jnp.minimum(position + 1, length) - base

    def homeward(way, k, stride):
        target = device(chip - (1 - 2 * way) * stride, core)
        return [
            pltpu.make_async_remote_copy(
                src_ref=stat.at[way, k],
                dst_ref=got_stat.at[way, k],
                send_sem=s_send.at[way, k],
                recv_sem=s_recv.at[way, k],
                device_id=target,
                device_id_type=MESH,
            ),
            pltpu.make_async_remote_copy(
                src_ref=send.at[way, k],
                dst_ref=got.at[way, k],
                send_sem=o_send.at[way, k],
                recv_sem=o_recv.at[way, k],
                device_id=target,
                device_id_type=MESH,
            ),
        ]

    def visit(k, unused):
        arrival(0, k).wait_recv()

        @pl.when(k < half)
        def _():
            arrival(1, k).wait_recv()

        for place, stride in enumerate(strides):
            turn = lax.rem(k, strides[max(place - 1, 0)]) == 0

            @pl.when(turn & (k + stride <= half))
            def _(stride=stride):
                relay(0, k, stride, q_all.at[0, k]).start()

            @pl.when(turn & (k + stride < half))
            def _(stride=stride):
                relay(1, k, stride, q_all.at[1, k]).start()

        rows = jnp.concatenate([q_all[0, k], q_all[1, k]], axis=0)
        mask = jnp.concatenate([pick[...], pick[...]], axis=1)
        rows = jnp.concatenate([rows * mask[0], rows * mask[1]], axis=1)
        back = lax.select(k == half, 0, k)
        limit = jnp.concatenate(
            [
                limit_of(lax.rem(chip - k + chips, chips)),
                limit_of(lax.rem(chip + back, chips)),
            ],
            axis=1,
        )
        numer, best, total = attend(keys, values_t, rows, limit)
        for way in (0, 1):
            here = slice(way * columns, (way + 1) * columns)
            mine = jnp.where(head_low, numer[:HEAD_DIM, here], numer[HEAD_DIM:, here])
            part[way, k] = mine
            send[way, k] = mine.astype(jnp.bfloat16)
            stat[way, k, 0:1] = best[:, here]
            stat[way, k, 1:2] = total[:, here]

        @pl.when(lax.rem(k, 2) == 1)
        def _():
            for way in (0, 1):
                for copy in homeward(way, k, 1):
                    copy.start()

        return unused

    lax.fori_loop(1, half + 1, visit, 0)
    for copy in homeward(0, half, strides[0]):
        copy.start()

    def own(way, k):
        return part[way, k], stat[way, k, 0:1], stat[way, k, 1:2]

    def received(way, k):
        for copy in homeward(way, k, 1):
            copy.wait_recv()
        return got[way, k], got_stat[way, k, 0:1], got_stat[way, k, 1:2]

    order = sorted(range(2, half, 2), key=lambda k: (step_of(k, strides), -k))
    for k in order:
        stride = step_of(k, strides)
        for way in (0, 1):
            children = [
                k + s
                for s in strides
                if s <= stride
                and k + s <= half - way
                and step_of(k + s, strides) == s
                and (s < stride or stride == strides[0])
            ]
            children.sort(key=lambda child: child - k)
            state = merge([own(way, k)] + [received(way, c) for c in children if c - k < strides[0]])
            for child in children:
                if child - k == strides[0]:
                    state = merge([state, received(way, child)])
            send[way, k] = state[0].astype(jnp.bfloat16)
            stat[way, k, 0:1] = state[1]
            stat[way, k, 1:2] = state[2]
            for copy in homeward(way, k, stride):
                copy.start()

    state = merge(
        [own(1, half)] + [received(way, s) for s in reversed(strides[1:]) for way in (0, 1)]
    )
    state = merge([state] + [received(way, strides[0]) for way in (0, 1)])
    merged = (state[0] / state[2]).T
    home[...] = merged.astype(jnp.bfloat16)
    their_half = pl.ds(pl.multiple_of(other * rows_half, 64), rows_half)
    back = to_partner(home.at[their_half], home_got, 3)
    back.start()
    out[core] = home[my_half]
    back.wait()
    out[other] = home_got[...]

    for way in (0, 1):
        for k in range(1, half + 1 - way):
            arrival(way, k).wait_send()
            for copy in homeward(way, k, 1):
                copy.wait_send()


def body(queries, keys, values, lengths, offsets):
    micro, local_rows, row_width = queries.shape
    shard, kv_width = keys.shape[1:]
    heads = row_width // HEAD_DIM
    chips = lax.axis_size("blk") // CORES
    half = chips // 2
    strides = (4, 2, 1)
    rows_half = local_rows * heads
    columns = CORES * rows_half
    packed = queries.reshape(micro, rows_half, HEAD_DIM)
    slots = (2, half + 1)
    dma = pltpu.SemaphoreType.DMA
    out = pl.pallas_call(
        functools.partial(kernel, chips, heads, strides),
        out_shape=jax.ShapeDtypeStruct((micro, rows_half, HEAD_DIM), jnp.bfloat16),
        in_specs=[
            pl.BlockSpec(memory_space=pltpu.SMEM),
            pl.BlockSpec(memory_space=pltpu.SMEM),
            pl.BlockSpec(memory_space=pl.ANY),
            pl.BlockSpec(memory_space=pl.ANY),
            pl.BlockSpec(memory_space=pl.ANY),
        ],
        out_specs=pl.BlockSpec(memory_space=pltpu.VMEM),
        scratch_shapes=[
            pltpu.VMEM((CORES * shard, kv_width), jnp.bfloat16),
            pltpu.VMEM((CORES * shard, kv_width), jnp.bfloat16),
            pltpu.VMEM((kv_width, CORES * shard), jnp.bfloat16),
            pltpu.VMEM((2, columns, HEAD_DIM), jnp.bfloat16),
            pltpu.VMEM(slots + (columns, HEAD_DIM), jnp.bfloat16),
            pltpu.VMEM(slots + (HEAD_DIM, columns), jnp.float32),
            pltpu.VMEM(slots + (8, columns), jnp.float32),
            pltpu.VMEM(slots + (HEAD_DIM, columns), jnp.bfloat16),
            pltpu.VMEM(slots + (HEAD_DIM, columns), jnp.bfloat16),
            pltpu.VMEM(slots + (8, columns), jnp.float32),
            pltpu.VMEM((columns, HEAD_DIM), jnp.bfloat16),
            pltpu.VMEM((rows_half, HEAD_DIM), jnp.bfloat16),
            dma((3,)),
            dma((4,)),
            dma((4,)),
            dma(slots),
            dma(slots),
            dma(slots),
            dma(slots),
            dma(slots),
            dma(slots),
        ],
        compiler_params=pltpu.CompilerParams(
            collective_id=0, has_side_effects=True, vmem_limit_bytes=48 * 2**20
        ),
        name="attend_all",
    )(lengths, offsets, packed, keys, values)
    return out.reshape(micro, local_rows, row_width)


def solution(mesh):
    return jax.shard_map(
        body,
        mesh=mesh,
        in_specs=(
            P("group", "blk", None),
            P("group", "blk", None),
            P("group", "blk", None),
            P("group"),
            P("group"),
        ),
        out_specs=P("group", "blk", None),
        check_vma=False,
    )
```

time: 482 us -> 121 us (0.25)
  waiting for transfers between devices: 346 us -> 0 us
  Pallas kernels: 0 us -> 116 us
  matrix products: 33.6 us -> 0 us
  local copies, waits for them, and re-layouts: 38.7 us -> 5.35 us
  other arithmetic: 26 us -> 0 us
  starting transfers between devices: 20.4 us -> 0 us
  between operations: 13.5 us -> 0.02 us
    all_to_all x2 -> x0, waiting for transfers between devices: 206 us -> none  [the longest x1 190 us: body(): lax.all_to_all(shaped_parts, 'blk', split_axis=1, concat_axis=1, tiled=True)]
    all_gather x1 -> x0, waiting for transfers between devices: 139 us -> none  [body(): visiting = lax.all_gather(queries, 'blk', axis=1, tiled=True)]
    pallas_call x0 -> x1, Pallas kernels: none -> 116 us  [body(): pl.pallas_call(functools.partial(kernel, chips, heads, strides), out_shap...]
    dot_general x8 -> x0, matrix products: 33.6 us -> none  [the longest x4 21.7 us: shard_partial(): jnp.einsum('bkgrs,bskd->bkgrd', weights.astype(jnp.bfloat16), value_split...]
    reduce_sum x6 -> x0, other arithmetic: 21.9 us -> none  [the longest x4 17.2 us: shard_partial(): totals = jnp.sum(weights, axis=-1)]
    all_to_all x2 -> x0, starting transfers between devices: 20.4 us -> none  [the longest x1 13.8 us: body(): lax.all_to_all(shaped_logs, 'blk', split_axis=1, concat_axis=1, tiled=True)]
    mul x2 -> x0, local copies, waits for them, and re-layouts: 8.37 us -> none  [body(): weighted = jnp.sum(split_parts * scales[..., None], axis=1)]
    dynamic_slice x8 -> x0, local copies, waits for them, and re-layouts: 7.96 us -> none  [the longest x4 5.63 us: one_block(): selected = lax.dynamic_slice_in_dim(visiting, block_start, block_rows, 1)]
  transfers between devices with their start and end apart: 3 -> 0, of which waited for: 3 -> 0; matrix products, arithmetic and copies ran while one was open for 5% -> 0% of each run, Pallas kernels for 0% -> 0%
where the time goes in v1:
time: 121 us
  Pallas kernels  116 us (96%)
  local copies, waits for them, and re-layouts  5.35 us (4%)
    pallas_call x1, Pallas kernels, body(): pl.pallas_call(functools.partial(kernel, chips, heads, strides), out_shap...  116 us
    unnamed x8, local copies, waits for them, and re-layouts  3.94 us

profile of v1, /device:TPU:37, one launch (start us, length us, event | category | flops | bytes accessed | tf_op | source)
XLA Modules:
  0.0 120.9 jit_solution(17001263755634792782)
XLA Ops:
  0.0 0.8 reshape.6.q_in
  0.8 0.0 copy-start
  0.8 1.3 %copy-done = bf16[2,1280,256]{2,1,0:T(8,128)(2,1)S(1)} copy-done((bf16[2,1280,256]{2,1,0:T(8,128)(2,1)S(1)}, bf16[2,1280,256]{2,1,0:T(8,128)(2,1)}, u32[]{:S(2)}) %copy-start) | copy-done | bytes 1310744
  2.1 0.0 copy-start.1
  2.1 1.3 %copy-done.1 = bf16[2,1280,256]{2,1,0:T(8,128)(2,1)S(1)} copy-done((bf16[2,1280,256]{2,1,0:T(8,128)(2,1)S(1)}, bf16[2,1280,256]{2,1,0:T(8,128)(2,1)}, u32[]{:S(2)}) %copy-start.1) | copy-done | bytes 1310744
  3.4 0.0 copy-start.2
  3.4 0.7 copy-done.2
  4.1 0.0 copy-start.3
  4.1 0.7 copy-done.3
  4.7 115.5 %attend_all.1 = bf16[2,64,128]{2,1,0:T(8,128)(2,1)S(1)} custom-call(s32[2]{0:T(128)S(1)} %copy-done.2, s32[2]{0:T(128)S(1)} %copy-done.3, bf16[2,64,128]{2,1,0:T(8,128)(2,1)S(1)} %reshape.6.q_in, bf16[2,1280,256]{2,1,0:T(8,128)(2,1)S(1)} %copy-done, bf16[2,1280,256]{2,1,0:T(8,128)(2,1)S(1)} %copy-done.1), custom_call_target="tpu_custom_call" | custom-call | tf_op jit(solution)/shard_map/attend_all/pallas_call | solution.py:329
  120.3 0.6 reshape.7
Async XLA Ops:
  0.8 1.3 %copy-start = (bf16[2,1280,256]{2,1,0:T(8,128)(2,1)S(1)}, bf16[2,1280,256]{2,1,0:T(8,128)(2,1)}, u32[]{:S(2)}) copy-start(bf16[2,1280,256]{2,1,0:T(8,128)(2,1)} %k_in.1) | copy-start | bytes 3932164
  2.1 1.3 %copy-start.1 = (bf16[2,1280,256]{2,1,0:T(8,128)(2,1)S(1)}, bf16[2,1280,256]{2,1,0:T(8,128)(2,1)}, u32[]{:S(2)}) copy-start(bf16[2,1280,256]{2,1,0:T(8,128)(2,1)} %v_in.1) | copy-start | bytes 3932164
  3.4 0.7 copy-start.2
  4.1 0.7 copy-start.3

commit v2 on v1

--- a/solution.py
+++ b/solution.py
@@ -15,13 +15,19 @@
 EXP_SCALE = math.log2(math.e) / math.sqrt(HEAD_DIM)
 LOW = -1e30
 TILE = 256
+PIECES = 1
 
 
 def step_of(distance, strides):
-    for stride in strides:
-        if distance % stride == 0:
-            return stride
-    return 1
+    return next(stride for stride in strides if distance % stride == 0)
+
+
+def fed_by(distance, furthest, strides):
+    return [
+        distance + stride
+        for stride in strides
+        if distance + stride <= furthest and step_of(distance + stride, strides) == stride
+    ]
 
 
 def merge(parts):
@@ -32,36 +38,34 @@
     return numer, best, total
 
 
-def attend(keys, values_t, rows, limit):
+def attend(keys, values_t, scores_ref, rows, limit, last_best):
     width = rows.shape[0]
     position = lax.broadcasted_iota(jnp.int32, (TILE, width), 0)
+    columns = rows.astype(jnp.float32).T.astype(jnp.bfloat16)
     best = numer = total = None
     for tile in range(keys.shape[0] // TILE):
         here = slice(tile * TILE, (tile + 1) * TILE)
-        scores = lax.dot_general(
-            keys[here, :], rows, (((1,), (1,)), ((), ())), preferred_element_type=jnp.float32
-        )
+        last = scores_ref[here, :]
+        scores = jnp.dot(keys[here, :], columns, preferred_element_type=jnp.float32)
         scores = jnp.where(position < limit - tile * TILE, scores, LOW)
-        largest = scores.reshape(TILE // 8, 8, width).max(0).max(0, keepdims=True)
-        newest = largest if best is None else jnp.maximum(best, largest)
-        weights = jnp.exp2((scores - newest) * EXP_SCALE)
+        largest = scores.reshape(TILE // 8, 8, width).max(0)
+        best = largest if best is None else jnp.maximum(best, largest)
+        weights = jnp.exp2((last - last_best) * EXP_SCALE)
+        scores_ref[here, :] = scores
         sums = weights.reshape(TILE // 8, 8, width).sum(0)
+        total = sums if total is None else total + sums
         product = jnp.dot(
             values_t[:, here], weights.astype(jnp.bfloat16), preferred_element_type=jnp.float32
         )
-        if best is None:
-            numer, total = product, sums
-        else:
-            keep = jnp.exp2((best - newest) * EXP_SCALE)
-            numer, total = numer * keep + product, total * keep + sums
-        best = newest
-    return numer, best, total.sum(0, keepdims=True)
+        numer = product if numer is None else numer + product
+    return best.max(0, keepdims=True), numer, total.sum(0, keepdims=True)
 
 
 def kernel(
     chips,
     heads,
-    strides,
+    gather_strides,
+    home_strides,
     lengths,
     offsets,
     q_in,
@@ -71,6 +75,7 @@
     keys,
     values,
     values_t,
+    scores,
     pick,
     q_all,
     part,
@@ -107,7 +112,8 @@
 
     barrier = pltpu.get_barrier_semaphore()
     pl.semaphore_signal(barrier, inc=1, device_id=partner, device_id_type=MESH)
-    for stride in strides:
+    peers = sorted(set(gather_strides + home_strides))
+    for stride in peers:
         for way in (-1, 1):
             pl.semaphore_signal(
                 barrier, inc=1, device_id=device(chip + way * stride, core), device_id_type=MESH
@@ -121,7 +127,7 @@
     ]
     for copy in locals_:
         copy.start()
-    pl.semaphore_wait(barrier, 1 + 2 * len(strides))
+    pl.semaphore_wait(barrier, 1 + 2 * len(peers))
 
     def to_partner(src, dst, index):
         return pltpu.make_async_remote_copy(
@@ -146,14 +152,13 @@
     pick[0] = low.astype(jnp.bfloat16)
     pick[1] = (1.0 - low).astype(jnp.bfloat16)
 
-    def relay(way, k, stride, src):
-        slot = k + stride
+    def relay(way, k, slot, src):
         return pltpu.make_async_remote_copy(
             src_ref=src,
             dst_ref=q_all.at[way, slot],
             send_sem=q_send.at[way, slot],
             recv_sem=q_recv.at[way, slot],
-            device_id=device(chip + (1 - 2 * way) * stride, core),
+            device_id=device(chip + (1 - 2 * way) * (slot - k), core),
             device_id_type=MESH,
         )
 
@@ -169,9 +174,9 @@
 
     locals_[0].wait()
     swaps[0].wait()
-    for stride in strides:
+    for slot in fed_by(0, half, gather_strides):
         for way in (0, 1):
-            relay(way, 0, stride, q_all.at[0, 0]).start()
+            relay(way, 0, slot, q_all.at[0, 0]).start()
     q_all[1, half] = q_all[0, 0]
 
     locals_[1].wait()
@@ -192,9 +197,12 @@
         position = offset + source * (columns // heads) + lax.div(column, heads)
         return jnp.minimum(position + 1, length) - base
 
-    def homeward(way, k, stride):
+    def pieces(k):
+        return PIECES if k % home_strides[0] == 0 else 1
+
+    def homeward(way, k, stride, count):
         target = device(chip - (1 - 2 * way) * stride, core)
-        return [
+        copies = [
             pltpu.make_async_remote_copy(
                 src_ref=stat.at[way, k],
                 dst_ref=got_stat.at[way, k],
@@ -202,35 +210,105 @@
                 recv_sem=s_recv.at[way, k],
                 device_id=target,
                 device_id_type=MESH,
-            ),
-            pltpu.make_async_remote_copy(
-                src_ref=send.at[way, k],
-                dst_ref=got.at[way, k],
-                send_sem=o_send.at[way, k],
-                recv_sem=o_recv.at[way, k],
-                device_id=target,
-                device_id_type=MESH,
-            ),
+            )
         ]
-
-    def visit(k, unused):
-        arrival(0, k).wait_recv()
-
-        @pl.when(k < half)
-        def _():
-            arrival(1, k).wait_recv()
-
-        for place, stride in enumerate(strides):
-            turn = lax.rem(k, strides[max(place - 1, 0)]) == 0
-
-            @pl.when(turn & (k + stride <= half))
-            def _(stride=stride):
-                relay(0, k, stride, q_all.at[0, k]).start()
-
-            @pl.when(turn & (k + stride < half))
-            def _(stride=stride):
-                relay(1, k, stride, q_all.at[1, k]).start()
-
+        size = HEAD_DIM // count
+        for piece in range(count):
+            span = pl.ds(piece * size, size)
+            copies.append(
+                pltpu.make_async_remote_copy(
+                    src_ref=send.at[way, k, span],
+                    dst_ref=got.at[way, k, span],
+                    send_sem=o_send.at[way, k, piece],
+                    recv_sem=o_recv.at[way, k, piece],
+                    device_id=target,
+                    device_id_type=MESH,
+                )
+            )
+        return copies
+
+    def own(way, k):
+        return part[way, k], stat[way, k, 0:1], stat[way, k, 1:2]
+
+    def received(way, k):
+        for copy in homeward(way, k, 1, pieces(k)):
+            copy.wait_recv()
+        return got[way, k], got_stat[way, k, 0:1], got_stat[way, k, 1:2]
+
+    def keep(way, k, state):
+        part[way, k] = state[0]
+        stat[way, k, 0:1] = state[1]
+        stat[way, k, 1:2] = state[2]
+
+    def gather(way, k):
+        nearby = [c for c in fed_by(k, half - way, home_strides) if c - k < home_strides[0]]
+        keep(way, k, merge([own(way, k)] + [received(way, c) for c in nearby]))
+
+    def forward(way, k):
+        stride = step_of(k, home_strides)
+        far = k + home_strides[0]
+        copies = homeward(way, k, stride, pieces(k))
+        if stride == home_strides[0] and far <= half - way:
+            coming = homeward(way, far, 1, PIECES)
+            coming[0].wait_recv()
+            best = jnp.maximum(stat[way, k, 0:1], got_stat[way, far, 0:1])
+            mine = jnp.exp2((stat[way, k, 0:1] - best) * EXP_SCALE)
+            theirs = jnp.exp2((got_stat[way, far, 0:1] - best) * EXP_SCALE)
+            stat[way, k, 0:1] = best
+            stat[way, k, 1:2] = stat[way, k, 1:2] * mine + got_stat[way, far, 1:2] * theirs
+            size = HEAD_DIM // PIECES
+            for piece in range(PIECES):
+                span = slice(piece * size, (piece + 1) * size)
+                coming[1 + piece].wait_recv()
+                joined = part[way, k, span] * mine + got[way, far, span] * theirs
+                send[way, k, span] = joined.astype(jnp.bfloat16)
+                if piece == 0:
+                    copies[0].start()
+                copies[1 + piece].start()
+        else:
+            send[way, k] = part[way, k].astype(jnp.bfloat16)
+            for copy in copies:
+                copy.start()
+
+    def ways(k):
+        return [way for way in (0, 1) if k <= half - way]
+
+    def await_block(way, k):
+        arrival(way, k).wait_recv()
+
+    top = gather_strides[0]
+    near = half - top
+
+    def chunk_at(turn):
+        return jnp.where(turn < near, turn + 1, half + near - turn)
+
+    scores[...] = jnp.zeros(scores.shape, scores.dtype)
+
+    def visit(turn, last_best):
+        for start in range(0, half, top):
+
+            @pl.when(turn == start)
+            def _(start=start):
+                k = start + top
+                for way in ways(k):
+                    await_block(way, k)
+                    if k + top <= half - way:
+                        relay(way, k, k + top, q_all.at[way, k]).start()
+                for slot in fed_by(k, half, gather_strides)[1:]:
+                    for way in ways(slot):
+                        relay(way, k, slot, q_all.at[way, k]).start()
+                for way in (0, 1):
+                    await_block(way, start + 2)
+                    relay(way, start + 2, start + 3, q_all.at[way, start + 2]).start()
+                for way in (0, 1):
+                    await_block(way, start + 1)
+
+            @pl.when(turn == (start + 1 if start == near else start + 2))
+            def _(start=start):
+                for way in (0, 1):
+                    await_block(way, start + 3)
+
+        k = chunk_at(jnp.minimum(turn, half - 1))
         rows = jnp.concatenate([q_all[0, k], q_all[1, k]], axis=0)
         mask = jnp.concatenate([pick[...], pick[...]], axis=1)
         rows = jnp.concatenate([rows * mask[0], rows * mask[1]], axis=1)
@@ -242,62 +320,54 @@
             ],
             axis=1,
         )
-        numer, best, total = attend(keys, values_t, rows, limit)
+        best, numer, total = attend(keys, values_t, scores, rows, limit, last_best)
+        done = chunk_at(jnp.maximum(turn - 1, 0))
         for way in (0, 1):
             here = slice(way * columns, (way + 1) * columns)
             mine = jnp.where(head_low, numer[:HEAD_DIM, here], numer[HEAD_DIM:, here])
-            part[way, k] = mine
-            send[way, k] = mine.astype(jnp.bfloat16)
-            stat[way, k, 0:1] = best[:, here]
-            stat[way, k, 1:2] = total[:, here]
-
-        @pl.when(lax.rem(k, 2) == 1)
+            keep(way, done, (mine, last_best[:, here], total[:, here]))
+            send[way, done] = mine.astype(jnp.bfloat16)
+
+        @pl.when((lax.rem(done, 2) == 1) & (turn > 0))
         def _():
             for way in (0, 1):
-                for copy in homeward(way, k, 1):
+                for copy in homeward(way, done, 1, 1):
                     copy.start()
 
-        return unused
-
-    lax.fori_loop(1, half + 1, visit, 0)
-    for copy in homeward(0, half, strides[0]):
-        copy.start()
-
-    def own(way, k):
-        return part[way, k], stat[way, k, 0:1], stat[way, k, 1:2]
-
-    def received(way, k):
-        for copy in homeward(way, k, 1):
-            copy.wait_recv()
-        return got[way, k], got_stat[way, k, 0:1], got_stat[way, k, 1:2]
-
-    order = sorted(range(2, half, 2), key=lambda k: (step_of(k, strides), -k))
+        @pl.when(turn == near + 1)
+        def _():
+            forward(0, half)
+
+        for start in range(0, near, top):
+
+            @pl.when(turn == start + top + 2)
+            def _(start=start):
+                for way in (0, 1):
+                    gather(way, start + 2)
+                    forward(way, start + 2)
+
+        return best
+
+    lax.fori_loop(0, half + 1, visit, jnp.zeros((1, 2 * columns), jnp.float32))
+
+    for way in (0, 1):
+        gather(way, near + 2)
+        forward(way, near + 2)
+    order = sorted(range(top, half, top), key=lambda k: (step_of(k, home_strides), -k))
     for k in order:
-        stride = step_of(k, strides)
         for way in (0, 1):
-            children = [
-                k + s
-                for s in strides
-                if s <= stride
-                and k + s <= half - way
-                and step_of(k + s, strides) == s
-                and (s < stride or stride == strides[0])
-            ]
-            children.sort(key=lambda child: child - k)
-            state = merge([own(way, k)] + [received(way, c) for c in children if c - k < strides[0]])
-            for child in children:
-                if child - k == strides[0]:
-                    state = merge([state, received(way, child)])
-            send[way, k] = state[0].astype(jnp.bfloat16)
-            stat[way, k, 0:1] = state[1]
-            stat[way, k, 1:2] = state[2]
-            for copy in homeward(way, k, stride):
-                copy.start()
-
+            gather(way, k)
+            forward(way, k)
     state = merge(
-        [own(1, half)] + [received(way, s) for s in reversed(strides[1:]) for way in (0, 1)]
+        [own(1, half)]
+        + [
+            received(way, s)
+            for s in fed_by(0, half, home_strides)
+            if s < home_strides[0]
+            for way in (0, 1)
+        ]
     )
-    state = merge([state] + [received(way, strides[0]) for way in (0, 1)])
+    state = merge([state] + [received(way, home_strides[0]) for way in (0, 1)])
     merged = (state[0] / state[2]).T
     home[...] = merged.astype(jnp.bfloat16)
     their_half = pl.ds(pl.multiple_of(other * rows_half, 64), rows_half)
@@ -310,7 +380,7 @@
     for way in (0, 1):
         for k in range(1, half + 1 - way):
             arrival(way, k).wait_send()
-            for copy in homeward(way, k, 1):
+            for copy in homeward(way, k, 1, pieces(k)):
                 copy.wait_send()
 
 
@@ -320,14 +390,13 @@
     heads = row_width // HEAD_DIM
     chips = lax.axis_size("blk") // CORES
     half = chips // 2
-    strides = (4, 2, 1)
     rows_half = local_rows * heads
     columns = CORES * rows_half
     packed = queries.reshape(micro, rows_half, HEAD_DIM)
     slots = (2, half + 1)
     dma = pltpu.SemaphoreType.DMA
     out = pl.pallas_call(
-        functools.partial(kernel, chips, heads, strides),
+        functools.partial(kernel, chips, heads, (4, 2, 1), (4, 2, 1)),
         out_shape=jax.ShapeDtypeStruct((micro, rows_half, HEAD_DIM), jnp.bfloat16),
         in_specs=[
             pl.BlockSpec(memory_space=pltpu.SMEM),
@@ -341,6 +410,7 @@
             pltpu.VMEM((CORES * shard, kv_width), jnp.bfloat16),
             pltpu.VMEM((CORES * shard, kv_width), jnp.bfloat16),
             pltpu.VMEM((kv_width, CORES * shard), jnp.bfloat16),
+            pltpu.VMEM((CORES * shard, 2 * columns), jnp.float32),
             pltpu.VMEM((2, columns, HEAD_DIM), jnp.bfloat16),
             pltpu.VMEM(slots + (columns, HEAD_DIM), jnp.bfloat16),
             pltpu.VMEM(slots + (HEAD_DIM, columns), jnp.float32),
@@ -355,8 +425,8 @@
             dma((4,)),
             dma(slots),
             dma(slots),
-            dma(slots),
-            dma(slots),
+            dma(slots + (PIECES,)),
+            dma(slots + (PIECES,)),
             dma(slots),
             dma(slots),
         ],

time: 121 us -> 104 us (0.86)
  Pallas kernels: 116 us -> 98.1 us
    pallas_call x1, Pallas kernels: 116 us -> 98.1 us  [body(): pl.pallas_call(functools.partial(kernel, chips, heads, (4, 2, 1), (4, 2,...]
where the time goes in v2:
time: 104 us; the launch traced here: 103 us
  Pallas kernels  98.1 us (94%)
  local copies, waits for them, and re-layouts  5.35 us (5%)
    pallas_call x1, Pallas kernels, body(): pl.pallas_call(functools.partial(kernel, chips, heads, (4, 2, 1), (4, 2,...  98.1 us
    unnamed x8, local copies, waits for them, and re-layouts  3.94 us

profile of v2, /device:TPU:37, one launch (start us, length us, event | category | flops | bytes accessed | tf_op | source)
XLA Modules:
  0.0 103.5 jit_solution(8255831952228560562)
XLA Ops:
  0.0 0.8 reshape.6.q_in
  0.8 0.0 copy-start
  0.8 1.3 %copy-done = bf16[2,1280,256]{2,1,0:T(8,128)(2,1)S(1)} copy-done((bf16[2,1280,256]{2,1,0:T(8,128)(2,1)S(1)}, bf16[2,1280,256]{2,1,0:T(8,128)(2,1)}, u32[]{:S(2)}) %copy-start) | copy-done | bytes 1310744
  2.1 0.0 copy-start.1
  2.1 1.3 %copy-done.1 = bf16[2,1280,256]{2,1,0:T(8,128)(2,1)S(1)} copy-done((bf16[2,1280,256]{2,1,0:T(8,128)(2,1)S(1)}, bf16[2,1280,256]{2,1,0:T(8,128)(2,1)}, u32[]{:S(2)}) %copy-start.1) | copy-done | bytes 1310744
  3.4 0.0 copy-start.2
  3.4 0.7 copy-done.2
  4.1 0.0 copy-start.3
  4.1 0.7 copy-done.3
  4.7 98.1 %attend_all.1 = bf16[2,64,128]{2,1,0:T(8,128)(2,1)S(1)} custom-call(s32[2]{0:T(128)S(1)} %copy-done.2, s32[2]{0:T(128)S(1)} %copy-done.3, bf16[2,64,128]{2,1,0:T(8,128)(2,1)S(1)} %reshape.6.q_in, bf16[2,1280,256]{2,1,0:T(8,128)(2,1)S(1)} %copy-done, bf16[2,1280,256]{2,1,0:T(8,128)(2,1)S(1)} %copy-done.1), custom_call_target="tpu_custom_call" | custom-call | tf_op jit(solution)/shard_map/attend_all/pallas_call | solution.py:398
  102.9 0.6 reshape.7
Async XLA Ops:
  0.8 1.3 %copy-start = (bf16[2,1280,256]{2,1,0:T(8,128)(2,1)S(1)}, bf16[2,1280,256]{2,1,0:T(8,128)(2,1)}, u32[]{:S(2)}) copy-start(bf16[2,1280,256]{2,1,0:T(8,128)(2,1)} %k_in.1) | copy-start | bytes 3932164
  2.1 1.3 %copy-start.1 = (bf16[2,1280,256]{2,1,0:T(8,128)(2,1)S(1)}, bf16[2,1280,256]{2,1,0:T(8,128)(2,1)}, u32[]{:S(2)}) copy-start(bf16[2,1280,256]{2,1,0:T(8,128)(2,1)} %v_in.1) | copy-start | bytes 3932164
  3.4 0.7 copy-start.2
  4.1 0.7 copy-start.3

commit v3 on v2

--- a/solution.py
+++ b/solution.py
@@ -77,6 +77,11 @@
     values_t,
     scores,
     pick,
+    k_stage,
+    v_stage,
+    q_raw,
+    wide,
+    packed,
     q_all,
     part,
     stat,
@@ -88,6 +93,7 @@
     local_sem,
     pair_send,
     pair_recv,
+    first_send,
     q_send,
     q_recv,
     o_send,
@@ -102,7 +108,8 @@
     other = 1 - core
     chip = lax.div(me, CORES)
     shard = k_in.shape[1]
-    rows_half = q_in.shape[1]
+    local_rows = q_in.shape[1]
+    rows_half = local_rows * heads
     columns = CORES * rows_half
 
     def device(z, on):
@@ -110,24 +117,37 @@
 
     partner = device(chip, other)
 
+    fetch = pltpu.make_async_copy(q_in, q_raw, local_sem.at[0])
+    fetch.start()
     barrier = pltpu.get_barrier_semaphore()
     pl.semaphore_signal(barrier, inc=1, device_id=partner, device_id_type=MESH)
     peers = sorted(set(gather_strides + home_strides))
     for stride in peers:
         for way in (-1, 1):
-            pl.semaphore_signal(
-                barrier, inc=1, device_id=device(chip + way * stride, core), device_id_type=MESH
-            )
+            for on in (0, 1):
+                pl.semaphore_signal(
+                    barrier, inc=1, device_id=device(chip + way * stride, on), device_id_type=MESH
+                )
     my_rows = pl.ds(pl.multiple_of(core * shard, 256), shard)
     my_half = pl.ds(pl.multiple_of(core * rows_half, 64), rows_half)
     locals_ = [
-        pltpu.make_async_copy(q_in.at[core], q_all.at[0, 0, my_half], local_sem.at[0]),
         pltpu.make_async_copy(v_in.at[core], values.at[my_rows], local_sem.at[1]),
         pltpu.make_async_copy(k_in.at[core], keys.at[my_rows], local_sem.at[2]),
+        pltpu.make_async_copy(v_in.at[other], v_stage, local_sem.at[3]),
+        pltpu.make_async_copy(k_in.at[other], k_stage, local_sem.at[4]),
     ]
     for copy in locals_:
         copy.start()
-    pl.semaphore_wait(barrier, 1 + 2 * len(peers))
+    fetch.wait()
+    for micro in (0, 1):
+        flat = q_raw[micro].astype(jnp.float32)
+        for head in range(heads):
+            wide[micro, pl.ds(head, local_rows, stride=heads)] = flat[
+                :, head * HEAD_DIM : (head + 1) * HEAD_DIM
+            ]
+        packed[micro] = wide[micro].astype(jnp.bfloat16)
+    q_all[1, half, my_half] = packed[core]
+    pl.semaphore_wait(barrier, 1 + 4 * len(peers))
 
     def to_partner(src, dst, index):
         return pltpu.make_async_remote_copy(
@@ -139,11 +159,31 @@
             device_id_type=MESH,
         )
 
+    def first(way, place, slot, on):
+        return pltpu.make_async_remote_copy(
+            src_ref=packed.at[on],
+            dst_ref=q_all.at[way, slot, my_half],
+            send_sem=first_send.at[way, place, on],
+            recv_sem=q_recv.at[way, slot],
+            device_id=device(chip + (1 - 2 * way) * slot, on),
+            device_id_type=MESH,
+        )
+
+    firsts = [
+        first(way, place, slot, on)
+        for place, slot in enumerate(fed_by(0, half, gather_strides))
+        for way in (0, 1)
+        for on in (0, 1)
+    ]
+    for copy in firsts:
+        copy.start()
     swaps = [
-        to_partner(q_in.at[other], q_all.at[0, 0, my_half], 0),
-        to_partner(v_in.at[other], values.at[my_rows], 1),
-        to_partner(k_in.at[other], keys.at[my_rows], 2),
+        to_partner(packed.at[other], q_all.at[1, half, my_half], 0),
+        to_partner(v_stage, values.at[my_rows], 1),
+        to_partner(k_stage, keys.at[my_rows], 2),
     ]
+    locals_[2].wait()
+    locals_[3].wait()
     for copy in swaps:
         copy.start()
 
@@ -172,21 +212,6 @@
             device_id_type=MESH,
         )
 
-    locals_[0].wait()
-    swaps[0].wait()
-    for slot in fed_by(0, half, gather_strides):
-        for way in (0, 1):
-            relay(way, 0, slot, q_all.at[0, 0]).start()
-    q_all[1, half] = q_all[0, 0]
-
-    locals_[1].wait()
-    swaps[1].wait()
-    for tile in range(values.shape[0] // TILE):
-        here = slice(tile * TILE, (tile + 1) * TILE)
-        values_t[:, here] = values[here, :].T
-    locals_[2].wait()
-    swaps[2].wait()
-
     length = lengths[core]
     offset = offsets[core]
     base = chip * CORES * shard
@@ -204,8 +229,8 @@
         target = device(chip - (1 - 2 * way) * stride, core)
         copies = [
             pltpu.make_async_remote_copy(
-                src_ref=stat.at[way, k],
-                dst_ref=got_stat.at[way, k],
+                src_ref=stat.at[way, k, pl.ds(0, 2)],
+                dst_ref=got_stat.at[way, k, pl.ds(0, 2)],
                 send_sem=s_send.at[way, k],
                 recv_sem=s_recv.at[way, k],
                 device_id=target,
@@ -282,26 +307,35 @@
     def chunk_at(turn):
         return jnp.where(turn < near, turn + 1, half + near - turn)
 
+    def relay_group(start):
+        k = start + top
+        for way in ways(k):
+            await_block(way, k)
+            if k + top <= half - way:
+                relay(way, k, k + top, q_all.at[way, k]).start()
+        for slot in fed_by(k, half, gather_strides)[1:]:
+            for way in ways(slot):
+                relay(way, k, slot, q_all.at[way, k]).start()
+        for way in (0, 1):
+            await_block(way, start + 2)
+            relay(way, start + 2, start + 3, q_all.at[way, start + 2]).start()
+        for way in (0, 1):
+            await_block(way, start + 1)
+
     scores[...] = jnp.zeros(scores.shape, scores.dtype)
-
+    relay_group(0)
+    locals_[0].wait()
+    swaps[1].wait()
+    for tile in range(values.shape[0] // TILE):
+        here = slice(tile * TILE, (tile + 1) * TILE)
+        values_t[:, here] = values[here, :].T
+    locals_[1].wait()
+    swaps[2].wait()
+    swaps[0].wait()
     def visit(turn, last_best):
         for start in range(0, half, top):
-
-            @pl.when(turn == start)
-            def _(start=start):
-                k = start + top
-                for way in ways(k):
-                    await_block(way, k)
-                    if k + top <= half - way:
-                        relay(way, k, k + top, q_all.at[way, k]).start()
-                for slot in fed_by(k, half, gather_strides)[1:]:
-                    for way in ways(slot):
-                        relay(way, k, slot, q_all.at[way, k]).start()
-                for way in (0, 1):
-                    await_block(way, start + 2)
-                    relay(way, start + 2, start + 3, q_all.at[way, start + 2]).start()
-                for way in (0, 1):
-                    await_block(way, start + 1)
+            if start:
+                pl.when(turn == start)(functools.partial(relay_group, start))
 
             @pl.when(turn == (start + 1 if start == near else start + 2))
             def _(start=start):
@@ -373,15 +407,25 @@
     their_half = pl.ds(pl.multiple_of(other * rows_half, 64), rows_half)
     back = to_partner(home.at[their_half], home_got, 3)
     back.start()
-    out[core] = home[my_half]
-    back.wait()
-    out[other] = home_got[...]
-
+
+    def unpack(micro, rows):
+        wide[0] = rows.astype(jnp.float32)
+        for head in range(heads):
+            out[micro, :, head * HEAD_DIM : (head + 1) * HEAD_DIM] = wide[
+                0, pl.ds(head, local_rows, stride=heads)
+            ].astype(jnp.bfloat16)
+
+    unpack(core, home[my_half])
+    for copy in firsts:
+        copy.wait_send()
     for way in (0, 1):
         for k in range(1, half + 1 - way):
-            arrival(way, k).wait_send()
+            if k not in fed_by(0, half, gather_strides):
+                arrival(way, k).wait_send()
             for copy in homeward(way, k, 1, pieces(k)):
                 copy.wait_send()
+    back.wait()
+    unpack(other, home_got[...])
 
 
 def body(queries, keys, values, lengths, offsets):
@@ -392,12 +436,11 @@
     half = chips // 2
     rows_half = local_rows * heads
     columns = CORES * rows_half
-    packed = queries.reshape(micro, rows_half, HEAD_DIM)
     slots = (2, half + 1)
     dma = pltpu.SemaphoreType.DMA
-    out = pl.pallas_call(
+    return pl.pallas_call(
         functools.partial(kernel, chips, heads, (4, 2, 1), (4, 2, 1)),
-        out_shape=jax.ShapeDtypeStruct((micro, rows_half, HEAD_DIM), jnp.bfloat16),
+        out_shape=jax.ShapeDtypeStruct(queries.shape, jnp.bfloat16),
         in_specs=[
             pl.BlockSpec(memory_space=pltpu.SMEM),
             pl.BlockSpec(memory_space=pltpu.SMEM),
@@ -412,6 +455,11 @@
             pltpu.VMEM((kv_width, CORES * shard), jnp.bfloat16),
             pltpu.VMEM((CORES * shard, 2 * columns), jnp.float32),
             pltpu.VMEM((2, columns, HEAD_DIM), jnp.bfloat16),
+            pltpu.VMEM((shard, kv_width), jnp.bfloat16),
+            pltpu.VMEM((shard, kv_width), jnp.bfloat16),
+            pltpu.VMEM(queries.shape, jnp.bfloat16),
+            pltpu.VMEM((micro, rows_half, HEAD_DIM), jnp.float32),
+            pltpu.VMEM((micro, rows_half, HEAD_DIM), jnp.bfloat16),
             pltpu.VMEM(slots + (columns, HEAD_DIM), jnp.bfloat16),
             pltpu.VMEM(slots + (HEAD_DIM, columns), jnp.float32),
             pltpu.VMEM(slots + (8, columns), jnp.float32),
@@ -420,9 +468,10 @@
             pltpu.VMEM(slots + (8, columns), jnp.float32),
             pltpu.VMEM((columns, HEAD_DIM), jnp.bfloat16),
             pltpu.VMEM((rows_half, HEAD_DIM), jnp.bfloat16),
-            dma((3,)),
+            dma((5,)),
             dma((4,)),
             dma((4,)),
+            dma((2, 3, CORES)),
             dma(slots),
             dma(slots),
             dma(slots + (PIECES,)),
@@ -431,11 +480,10 @@
             dma(slots),
         ],
         compiler_params=pltpu.CompilerParams(
-            collective_id=0, has_side_effects=True, vmem_limit_bytes=48 * 2**20
+            collective_id=0, has_side_effects=True, vmem_limit_bytes=63 * 2**20
         ),
         name="attend_all",
-    )(lengths, offsets, packed, keys, values)
-    return out.reshape(micro, local_rows, row_width)
+    )(lengths, offsets, queries, keys, values)
 
 
 def solution(mesh):

time: 104 us -> 100 us (0.962)
  local copies, waits for them, and re-layouts: 5.35 us -> 1.39 us
    unnamed x8 -> x1, local copies, waits for them, and re-layouts: 3.94 us -> 1.39 us
    reshape x2 -> x0, local copies, waits for them, and re-layouts: 1.41 us -> none  [the longest x1 0.78 us: body(): packed = queries.reshape(micro, rows_half, HEAD_DIM)]
where the time goes in v3:
time: 100 us
  Pallas kernels  98.7 us (99%)
  local copies, waits for them, and re-layouts  1.39 us (1%)
    pallas_call x1, Pallas kernels, body(): pl.pallas_call(functools.partial(kernel, chips, heads, (4, 2, 1), (4, 2,...  98.7 us

profile of v3, /device:TPU:37, one launch (start us, length us, event | category | flops | bytes accessed | tf_op | source)
XLA Modules:
  0.0 100.1 jit_solution(11096801741014099058)
XLA Ops:
  0.0 98.7 %attend_all.1 = bf16[2,4,2048]{2,1,0:T(4,128)(2,1)} custom-call(s32[2]{0:T(128)} %lengths.1, s32[2]{0:T(128)} %offsets.1, bf16[2,4,2048]{2,1,0:T(4,128)(2,1)} %q_in.1, bf16[2,1280,256]{2,1,0:T(8,128)(2,1)} %k_in.1, bf16[2,1280,256]{2,1,0:T(8,128)(2,1)} %v_in.1), custom_call_target="tpu_custom_call" | custom-call | tf_op jit(solution)/shard_map/attend_all/pallas_call | solution.py:441
  98.7 1.4 %copy.7 = bf16[2,4,2048]{2,1,0:T(4,128)(2,1)} copy(bf16[2,4,2048]{2,1,0:T(4,128)(2,1)} %attend_all.1) | data formatting | bytes 65536

commit v4 on v3

--- a/solution.py
+++ b/solution.py
@@ -80,6 +80,7 @@
     k_stage,
     v_stage,
     q_raw,
+    out_raw,
     wide,
     packed,
     q_all,
@@ -117,7 +118,7 @@
 
     partner = device(chip, other)
 
-    fetch = pltpu.make_async_copy(q_in, q_raw, local_sem.at[0])
+    fetch = pltpu.make_async_copy(q_in, q_raw.at[pl.ds(0, CORES)], local_sem.at[0])
     fetch.start()
     barrier = pltpu.get_barrier_semaphore()
     pl.semaphore_signal(barrier, inc=1, device_id=partner, device_id_type=MESH)
@@ -411,7 +412,7 @@
     def unpack(micro, rows):
         wide[0] = rows.astype(jnp.float32)
         for head in range(heads):
-            out[micro, :, head * HEAD_DIM : (head + 1) * HEAD_DIM] = wide[
+            out_raw[micro, :, head * HEAD_DIM : (head + 1) * HEAD_DIM] = wide[
                 0, pl.ds(head, local_rows, stride=heads)
             ].astype(jnp.bfloat16)
 
@@ -426,6 +427,9 @@
                 copy.wait_send()
     back.wait()
     unpack(other, home_got[...])
+    store = pltpu.make_async_copy(out_raw.at[pl.ds(0, CORES)], out, local_sem.at[0])
+    store.start()
+    store.wait()
 
 
 def body(queries, keys, values, lengths, offsets):
@@ -448,7 +452,7 @@
             pl.BlockSpec(memory_space=pl.ANY),
             pl.BlockSpec(memory_space=pl.ANY),
         ],
-        out_specs=pl.BlockSpec(memory_space=pltpu.VMEM),
+        out_specs=pl.BlockSpec(memory_space=pl.ANY),
         scratch_shapes=[
             pltpu.VMEM((CORES * shard, kv_width), jnp.bfloat16),
             pltpu.VMEM((CORES * shard, kv_width), jnp.bfloat16),
@@ -457,8 +461,9 @@
             pltpu.VMEM((2, columns, HEAD_DIM), jnp.bfloat16),
             pltpu.VMEM((shard, kv_width), jnp.bfloat16),
             pltpu.VMEM((shard, kv_width), jnp.bfloat16),
-            pltpu.VMEM(queries.shape, jnp.bfloat16),
-            pltpu.VMEM((micro, rows_half, HEAD_DIM), jnp.float32),
+            pltpu.VMEM((micro + 2, local_rows, row_width), jnp.bfloat16),
+            pltpu.VMEM((micro + 2, local_rows, row_width), jnp.bfloat16),
+            pltpu.VMEM((micro + 2, rows_half, HEAD_DIM), jnp.float32),
             pltpu.VMEM((micro, rows_half, HEAD_DIM), jnp.bfloat16),
             pltpu.VMEM(slots + (columns, HEAD_DIM), jnp.bfloat16),
             pltpu.VMEM(slots + (HEAD_DIM, columns), jnp.float32),

time: 100 us -> 100 us (level)
  no operation moved by 1% of the time
where the time goes in v4:
time: 100 us
  Pallas kernels  98.7 us (99%)
  local copies, waits for them, and re-layouts  1.39 us (1%)
    pallas_call x1, Pallas kernels, body(): pl.pallas_call(functools.partial(kernel, chips, heads, (4, 2, 1), (4, 2,...  98.7 us

profile of v4, /device:TPU:37, one launch (start us, length us, event | category | flops | bytes accessed | tf_op | source)
XLA Modules:
  0.0 100.1 jit_solution(7575416144651690632)
XLA Ops:
  0.0 98.7 %attend_all.1 = bf16[2,4,2048]{2,1,0:T(4,128)(2,1)} custom-call(s32[2]{0:T(128)} %lengths.1, s32[2]{0:T(128)} %offsets.1, bf16[2,4,2048]{2,1,0:T(4,128)(2,1)} %q_in.1, bf16[2,1280,256]{2,1,0:T(8,128)(2,1)} %k_in.1, bf16[2,1280,256]{2,1,0:T(8,128)(2,1)} %v_in.1), custom_call_target="tpu_custom_call" | custom-call | tf_op jit(solution)/shard_map/attend_all/pallas_call | solution.py:445
  98.7 1.4 %copy.7 = bf16[2,4,2048]{2,1,0:T(4,128)(2,1)} copy(bf16[2,4,2048]{2,1,0:T(4,128)(2,1)} %attend_all.1) | data formatting | bytes 65536
